TPU v7x, 32 devices: a whole 2x2x4 slice. The times are simulated.
32 devices in a mesh: depth: 2 (over core), rows: 4 (over y, x), cols: 4 (over z).
Axes of the slice: x: 2, y: 2, z: 4, core: 2. Of those that a mesh axis runs over, the one named last changes fastest.
Arguments:
- section_states: float32 [2, 128, 64, 256], P('depth', 'rows', 'cols'), may hold values from -6 to 6
- weights: bfloat16 [4, 3, 3, 256, 256], P('depth'), may hold values from -0.125 to 0.125
Outputs:
- fine_states: float32 [4, 128, 64, 256], P('depth', 'rows', 'cols')
- coarse_states: float32 [2, 128, 64, 256], P('depth', 'rows', 'cols')
All inputs are finite; a program needn't handle non-finite values.
Results may differ from a plain program's by a relative error of at most 0.002.
Values may be sent and summed in bfloat16 or wider, within the bound.
A program may use at most 64 MiB of HBM per device.

v0:
```python
import functools

import jax
import jax.numpy as jnp
from jax import lax
from jax.experimental import pallas as pl
from jax.experimental.pallas import tpu as pltpu
from jax.sharding import PartitionSpec as P

MESH = pl.DeviceIdType.MESH
HALO = 4
LANES = 128
LIMIT = 32 * 1024 * 1024


def padded_2(shard, sides, width):
    for axis, dim in sides:
        size, length = (lax.axis_size(axis), shard.shape[dim])
        up = [(i, (i + 1) % size) for i in range(size - 1)]
        down = [(j, i) for i, j in up]
        last = lax.slice_in_dim(shard, length - width, length, axis=dim)
        initial = lax.slice_in_dim(shard, 0, width, axis=dim)
        before = lax.ppermute(last, axis, up)
        after = lax.ppermute(initial, axis, down)
        shard = jnp.concatenate([before, shard, after], axis=dim)
    return shard


def shifted_2(block, axis, distance):
    devices = range(lax.axis_size(axis))
    route = [(i - distance, i) for i in devices if i - distance in devices]
    return lax.ppermute(block, axis, route)


def activate(field):
    return jax.nn.silu(field).astype(jnp.bfloat16)


def apply_stencil(padded, flat_weight, out_rows, out_cols):
    channels = padded.shape[2]
    patches = jnp.concatenate(
        [
            padded[shift_row : shift_row + out_rows, shift_col : shift_col + out_cols]
            for shift_row in range(3)
            for shift_col in range(3)
        ],
        axis=2,
    )
    summed = jnp.dot(
        patches.reshape(out_rows * out_cols, 9 * channels),
        flat_weight,
        preferred_element_type=jnp.float32,
    )
    return summed.reshape(out_rows, out_cols, channels)


def section_pass(anchor, first_weight, second_weight, step_size):
    rows_here, cols_here, channels = anchor.shape
    widened = padded_2(anchor, (("rows", 0), ("cols", 1)), 2)
    slope_wide = apply_stencil(activate(widened), first_weight, rows_here + 2, cols_here + 2)
    middle_wide = widened[1:-1, 1:-1] + step_size * slope_wide
    row_global = lax.axis_index("rows") * rows_here - 1 + jnp.arange(rows_here + 2)
    col_global = lax.axis_index("cols") * cols_here - 1 + jnp.arange(cols_here + 2)
    inside_rows = (row_global >= 0) & (row_global < rows_here * lax.axis_size("rows"))
    inside_cols = (col_global >= 0) & (col_global < cols_here * lax.axis_size("cols"))
    inside = inside_rows[:, None] & inside_cols[None, :]
    second_act = jnp.where(inside[:, :, None], activate(middle_wide), jnp.zeros((), jnp.bfloat16))
    first_slope = slope_wide[1:-1, 1:-1]
    middle = middle_wide[1:-1, 1:-1]
    second_slope = apply_stencil(second_act, second_weight, rows_here, cols_here)
    ending = middle + step_size * second_slope
    return (first_slope, middle, ending)


def chain_on_device(section_states, weights):
    rows_here, cols_here, channels = section_states.shape[1:]
    ndepth = lax.axis_size("depth")
    position = lax.axis_index("depth")
    step_size = 2.0 / (2 * ndepth)
    first_weight = weights[0].reshape(9 * channels, channels)
    second_weight = weights[1].reshape(9 * channels, channels)
    anchor = section_states[0]
    first_slope, middle, ending = section_pass(anchor, first_weight, second_weight, step_size)
    jump = ending - (anchor + 2.0 * step_size * first_slope)

    def chain_turn(step_index, current):
        padded = padded_2(activate(current), (("rows", 0), ("cols", 1)), 1)
        advanced = (
            current
            + 2.0 * step_size * apply_stencil(padded, first_weight, rows_here, cols_here)
            + jump
        )
        shifted = shifted_2(advanced, "depth", 1)
        return jnp.where(position == 0, anchor, shifted)

    corrected = lax.fori_loop(0, ndepth - 1, chain_turn, anchor)
    final_slope, final_middle, final_ending = section_pass(
        corrected, first_weight, second_weight, step_size
    )
    fine_states = jnp.stack([final_middle, final_ending])
    return (fine_states, corrected[None])


def largest_divisor(total, limit):
    return max(n for n in range(1, limit + 1) if total % n == 0)


DIRECTIONS = ((-1, 0), (1, 0), (0, -1), (0, 1), (-1, -1), (-1, 1), (1, -1), (1, 1))


def cycle_kernel(
    sizes, x_hbm, w_hbm, act1, w_last, stage,
    w_first, base, mid, end, act0, inside,
    flat, send_row, send_col, recv_row, recv_col, recv_corner,
    load_sem, send_sem, recv_sem, pass_send, pass_recv,
):
    nrows, ncols, step_size = sizes
    x = stage.at[2]
    w = (w_first, w_last)
    rows_here, cols_here, channels = x.shape
    halves = channels // LANES
    high, wide = rows_here + 2 * HALO, cols_here + 2 * HALO
    depth, row, col = lax.axis_index("depth"), lax.axis_index("rows"), lax.axis_index("cols")

    x_load = pltpu.make_async_copy(x_hbm.at[0], x, load_sem.at[0])
    w_loads = [pltpu.make_async_copy(w_hbm.at[k], w[k], load_sem.at[1 + k]) for k in range(2)]

    barrier = pltpu.get_barrier_semaphore()

    def neighbour(step):
        there_row, there_col = row + step[0], col + step[1]
        exists = (there_row >= 0) & (there_row < nrows) & (there_col >= 0) & (there_col < ncols)
        return exists, (depth, there_row, there_col)

    @pl.when(depth == 0)
    def _():
        x_load.start()

    for copy in w_loads:
        copy.start()
    pl.semaphore_signal(barrier, inc=1, device_id=(1 - depth, row, col), device_id_type=MESH)

    @pl.when(depth == 0)
    def _():
        for step in DIRECTIONS:
            exists, target = neighbour(step)

            @pl.when(exists)
            def _():
                pl.semaphore_signal(barrier, inc=1, device_id=target, device_id_type=MESH)

    def halves_of(c):
        return pl.ds(c * LANES, LANES)

    def silu(u):
        half = 0.5 * u
        return half + half * jnp.tanh(half)

    def masked_silu(u, first_row):
        half = 0.5 * u
        kept = half * inside[pl.ds(first_row, u.shape[0])]
        return kept + kept * jnp.tanh(half)

    def mark_inside(k, _):
        i = lax.broadcasted_iota(jnp.int32, (1, wide, LANES), 0) + (row * rows_here - HALO + k)
        j = lax.broadcasted_iota(jnp.int32, (1, wide, LANES), 1) + (col * cols_here - HALO)
        held = (i >= 0) & (i < nrows * rows_here) & (j >= 0) & (j < ncols * cols_here)
        inside[pl.ds(k, 1)] = jnp.where(held, 1.0, 0.0)
        return 0

    lax.fori_loop(0, high, mark_inside, 0, unroll=4)

    def slopes(act, layer, groups):
        lhs = []
        for a in range(3):
            for b in range(3):
                for c in range(halves):
                    parts = [
                        act[c, pl.ds(first_row + a - 1, n), b : b + wide, :]
                        .reshape(n * wide, LANES).astype(jnp.bfloat16)
                        for first_row, n in groups
                    ]
                    lhs.append(parts[0] if len(parts) == 1 else jnp.concatenate(parts, axis=0))
        acc = jnp.dot(jnp.concatenate(lhs, axis=1), w[layer][...], preferred_element_type=jnp.float32)
        rises = []
        filled = 0
        for _, n in groups:
            rise = step_size * acc[filled : filled + n * wide]
            rises.append(
                [rise[:, c * LANES : (c + 1) * LANES].reshape(n, wide, LANES) for c in range(halves)]
            )
            filled += n * wide
        return rises

    def stage_interior(state, slot):
        def body(i, _):
            for c in range(halves):
                stage[slot, i, :, halves_of(c)] = state[c, i + HALO, HALO : HALO + cols_here, :]
            return 0

        lax.fori_loop(0, rows_here, body, 0, unroll=4)

    end_rows = high - 4
    piece = largest_divisor(end_rows, 9)
    pieces = end_rows // piece

    def hand_over(k):
        rows = pl.ds(2 + k * piece, piece)
        return pltpu.make_async_remote_copy(
            src_ref=end.at[:, rows], dst_ref=end.at[:, rows],
            send_sem=pass_send.at[k], recv_sem=pass_recv.at[k],
            device_id=(1 - depth, row, col), device_id_type=MESH,
        )

    def first_layer(source, groups):
        for (at, n), rise in zip(groups, slopes(act0, 0, groups)):
            for c in range(halves):
                u = source[c, pl.ds(at, n)] + rise[c]
                mid[c, pl.ds(at, n)] = u
                act1[c, pl.ds(at, n), 1 : 1 + wide, :] = masked_silu(u, at)

    @pl.when(depth == 0)
    def _():
        def clear(i, _):
            for c in range(halves):
                base[c, pl.ds(i, 1)] = jnp.zeros((1, wide, LANES), jnp.float32)
                act0[c, pl.ds(i, 1)] = jnp.zeros((1,) + act0.shape[2:], jnp.float32)
            return 0

        lax.fori_loop(0, high, clear, 0, unroll=4)
        x_load.wait()
        for side in range(2):
            rows_from = 0 if side == 0 else rows_here - HALO
            cols_from = 0 if side == 0 else cols_here - HALO
            send_row[side] = (
                x[rows_from : rows_from + HALO].reshape(HALO * cols_here, channels).astype(jnp.bfloat16)
            )
            for i in range(rows_here):
                for c in range(halves):
                    flat[side, c, i * HALO : (i + 1) * HALO, :] = x[
                        i, cols_from : cols_from + HALO, c * LANES : (c + 1) * LANES
                    ]
            for c in range(halves):
                send_col[side, :, halves_of(c)] = flat[side, c].astype(jnp.bfloat16)
        peers = jnp.int32(1)
        for step in DIRECTIONS:
            exists, target = neighbour(step)
            peers = peers + jnp.where(exists, 1, 0)
        pl.semaphore_wait(barrier, peers)

        corner = HALO * HALO
        copies = []
        for k, (dr, dc) in enumerate(DIRECTIONS):
            exists, target = neighbour((dr, dc))
            if dc == 0:
                side = (dr + 1) // 2
                src, dst = send_row.at[side], recv_row.at[1 - side]
            elif dr == 0:
                side = (dc + 1) // 2
                src, dst = send_col.at[side], recv_col.at[1 - side]
            else:
                side = (dc + 1) // 2
                from_row = 0 if dr < 0 else (rows_here - HALO) * HALO
                src = send_col.at[side, pl.ds(from_row, corner)]
                dst = recv_corner.at[(1 - dr) // 2, (1 - dc) // 2]
            opposite = DIRECTIONS.index((-dr, -dc))
            copy = pltpu.make_async_remote_copy(
                src_ref=src, dst_ref=dst, send_sem=send_sem.at[k], recv_sem=recv_sem.at[opposite],
                device_id=target, device_id_type=MESH,
            )
            arrival = pltpu.make_async_remote_copy(
                src_ref=src,
                dst_ref=(
                    recv_row.at[(dr + 1) // 2] if dc == 0
                    else recv_col.at[(dc + 1) // 2] if dr == 0
                    else recv_corner.at[(dr + 1) // 2, (dc + 1) // 2]
                ),
                send_sem=send_sem.at[k], recv_sem=recv_sem.at[k],
                device_id=target, device_id_type=MESH,
            )
            copies.append((exists, copy, arrival))
        order = (4, 5, 6, 7, 2, 3, 0, 1)
        for k in order:
            exists, copy, arrival = copies[k]
            pl.when(exists)(copy.start)

        def place(i, _):
            for c in range(halves):
                u = x[i, :, halves_of(c)]
                base[c, i + HALO, HALO : HALO + cols_here, :] = u
                act0[c, i + HALO, HALO + 1 : HALO + 1 + cols_here, :] = silu(u)
            return 0

        lax.fori_loop(0, rows_here, place, 0, unroll=4)

        def put(c, i, j, u, act):
            base[c, i, j : j + u.shape[0], :] = u
            act0[c, i, j + 1 : j + 1 + u.shape[0], :] = act

        def take(k):
            exists, copy, arrival = copies[k]
            dr, dc = DIRECTIONS[k]

            @pl.when(exists)
            def _(arrival=arrival, dr=dr, dc=dc):
                arrival.wait_recv()
                top = {-1: 0, 0: HALO, 1: high - HALO}[dr]
                left = {-1: 0, 0: HALO, 1: wide - HALO}[dc]
                for c in range(halves):
                    if dr == 0:
                        side = (dc + 1) // 2
                        u = recv_col[side, :, halves_of(c)].astype(jnp.float32)
                        flat[0, c] = u
                        flat[1, c] = silu(u)
                        for i in range(rows_here):
                            part = slice(i * HALO, (i + 1) * HALO)
                            put(c, top + i, left, flat[0, c, part, :], flat[1, c, part, :])
                        continue
                    if dc == 0:
                        u = recv_row[(dr + 1) // 2, :, halves_of(c)].astype(jnp.float32)
                    else:
                        u = recv_corner[(dr + 1) // 2, (dc + 1) // 2, :, halves_of(c)].astype(jnp.float32)
                    act, n = silu(u), u.shape[0] // HALO
                    for i in range(HALO):
                        part = slice(i * n, (i + 1) * n)
                        put(c, top + i, left, u[part], act[part])

        w_loads[0].wait()
        for k in (2, 3, 0, 1, 4, 5, 6, 7):
            take(k)
        first_layer(base, [(1, high - 2)])
        stage_interior(mid, 0)
        w_loads[1].wait()

        def second(k, _):
            at = 2 + k * piece
            rise = slopes(act1, 1, [(at, piece)])[0]
            for c in range(halves):
                end[c, pl.ds(at, piece)] = mid[c, pl.ds(at, piece)] + rise[c]
            hand_over(k).start()
            return 0

        lax.fori_loop(0, pieces, second, 0)
        stage_interior(end, 1)
        for exists, copy, arrival in copies:

            @pl.when(exists)
            def _(copy=copy):
                copy.wait_send()

        def sent(k, _):
            hand_over(k).wait_send()
            return 0

        lax.fori_loop(0, pieces, sent, 0)

    @pl.when(depth == 1)
    def _():
        pl.semaphore_wait(barrier, 1)

        w_loads[0].wait()

        def received(k, _):
            hand_over(k).wait_recv()
            at = 2 + k * piece
            for c in range(halves):
                u = end[c, pl.ds(at, piece)]
                act0[c, pl.ds(at, piece), 1 : 1 + wide, :] = masked_silu(u, at)
            first_layer(end, [(at - 1, piece)])
            return 0

        lax.fori_loop(0, pieces, received, 0)
        stage_interior(end, 2)
        stage_interior(mid, 0)
        w_loads[1].wait()


def last_kernel(
    step_size, act, w, stage, fine_hbm, coarse_hbm, ending, store_sem, piece_sem
):
    _, rows_here, cols_here, channels = stage.shape
    halves = channels // LANES
    depth = lax.axis_index("depth")
    pieces = piece_sem.shape[0]
    n = rows_here // pieces
    m = n * cols_here

    def store(slot, ref):
        return pltpu.make_async_copy(stage.at[slot], ref, store_sem.at[slot])

    coarse_store = store(2, coarse_hbm.at[0])
    first_store = store(0, fine_hbm.at[0])
    coarse_store.start()
    first_store.start()

    @pl.when(depth == 0)
    def _():
        second_store = store(1, fine_hbm.at[1])
        second_store.start()
        second_store.wait()

    @pl.when(depth == 1)
    def _():
        def piece_store(k):
            rows = pl.ds(k * n, n)
            return pltpu.make_async_copy(ending.at[rows], fine_hbm.at[1, rows], piece_sem.at[k])

        def last(k):
            at = k * n
            lhs = [
                act[c, pl.ds(at + HALO + a - 1, n), HALO + b : HALO + b + cols_here, :]
                .reshape(m, LANES).astype(jnp.bfloat16)
                for a in range(3) for b in range(3) for c in range(halves)
            ]
            acc = jnp.dot(jnp.concatenate(lhs, axis=1), w[...], preferred_element_type=jnp.float32)
            ending[pl.ds(at, n)] = stage[0, pl.ds(at, n)] + step_size * acc.reshape(n, cols_here, channels)
            piece_store(k).start()

        for k in range(pieces):
            last(k)
        for k in range(pieces):
            piece_store(k).wait()

    coarse_store.wait()
    first_store.wait()


def two_sections(section_states, weights):
    _, rows_here, cols_here, channels = section_states.shape
    halves = channels // LANES
    high, wide = rows_here + 2 * HALO, cols_here + 2 * HALO
    act_wide = -(-(wide + 2) // 8) * 8
    pieces = (high - 4) // largest_divisor(high - 4, 9)
    sizes = (lax.axis_size("rows"), lax.axis_size("cols"), 2.0 / (2 * lax.axis_size("depth")))
    f32, bf16, vmem = jnp.float32, jnp.bfloat16, pltpu.VMEM
    state = vmem((halves, high, wide, LANES), f32)
    act = vmem((halves, high, act_wide, LANES), f32)
    flat_weights = weights.reshape(2, 9 * channels, channels)
    any_space, in_vmem = pl.BlockSpec(memory_space=pl.ANY), pl.BlockSpec(memory_space=vmem)
    act_last, w_last, stage = pl.pallas_call(
        functools.partial(cycle_kernel, sizes),
        out_shape=(
            act,
            vmem((9 * channels, channels), bf16),
            vmem((3, rows_here, cols_here, channels), f32),
        ),
        in_specs=[pl.BlockSpec(memory_space=pltpu.HBM)] * 2,
        out_specs=[in_vmem] * 3,
        scratch_shapes=[
            vmem((9 * channels, channels), bf16),
            state, state, state, act,
            vmem((high, wide, LANES), f32),
            vmem((2, halves, rows_here * HALO, LANES), f32),
            vmem((2, HALO * cols_here, channels), bf16),
            vmem((2, rows_here * HALO, channels), bf16),
            vmem((2, HALO * cols_here, channels), bf16),
            vmem((2, rows_here * HALO, channels), bf16),
            vmem((2, 2, HALO * HALO, channels), bf16),
            pltpu.SemaphoreType.DMA((3,)),
            pltpu.SemaphoreType.DMA((8,)),
            pltpu.SemaphoreType.DMA((8,)),
            pltpu.SemaphoreType.DMA((pieces,)),
            pltpu.SemaphoreType.DMA((pieces,)),
        ],
        compiler_params=pltpu.CompilerParams(
            collective_id=0, has_side_effects=True, vmem_limit_bytes=LIMIT
        ),
    )(
        pltpu.with_memory_space_constraint(section_states, pltpu.HBM),
        pltpu.with_memory_space_constraint(flat_weights, pltpu.HBM),
    )
    last_pieces = rows_here // largest_divisor(rows_here, 8)
    return pl.pallas_call(
        functools.partial(last_kernel, sizes[2]),
        out_shape=(
            jax.ShapeDtypeStruct((2, rows_here, cols_here, channels), f32),
            jax.ShapeDtypeStruct((1, rows_here, cols_here, channels), f32),
        ),
        in_specs=[in_vmem] * 3,
        out_specs=[any_space] * 2,
        scratch_shapes=[
            vmem((rows_here, cols_here, channels), f32),
            pltpu.SemaphoreType.DMA((3,)),
            pltpu.SemaphoreType.DMA((last_pieces,)),
        ],
        compiler_params=pltpu.CompilerParams(vmem_limit_bytes=LIMIT),
    )(act_last, w_last, stage)


def on_device(section_states, weights):
    _, rows_here, cols_here, channels = section_states.shape
    tiles = rows_here % 8 == 0 and cols_here % 8 == 0 and channels % LANES == 0
    if lax.axis_size("depth") == 2 and tiles and min(rows_here, cols_here) >= HALO:
        return two_sections(section_states, weights)
    return chain_on_device(section_states, weights)


def solution(mesh):
    in_specs = (P("depth", "rows", "cols", None), P("depth", None, None, None, None))
    out_specs = (P("depth", "rows", "cols", None), P("depth", "rows", "cols", None))
    return jax.shard_map(
        on_device, mesh=mesh, in_specs=in_specs, out_specs=out_specs, check_vma=False
    )
```

profile of v0, /device:TPU:1, one launch (start us, length us, event | category | flops | bytes accessed | tf_op | source)
XLA Modules:
  0.0 15.5 jit_solution(12884937142414031788)
XLA Ops:
  0.6 13.3 %shard_map.41 = (f32[2,40,32,128]{3,2,1,0:T(8,128)S(1)}, bf16[2304,256]{1,0:T(8,128)(2,1)S(1)}, f32[3,32,16,256]{3,2,1,0:T(8,128)S(1)}) custom-call(f32[1,32,16,256]{3,2,1,0:T(8,128)} %x_hbm.1, bf16[2,2304,256]{2,1,0:T(8,128)(2,1)} %bitcast.1), custom_call_target="tpu_custom_call" | custom-call | tf_op jit(solution)/shard_map/pallas_call | solution.py:440
  13.9 1.6 %shard_map.42 = (f32[2,32,16,256]{3,2,1,0:T(8,128)}, f32[1,32,16,256]{3,2,1,0:T(8,128)}) custom-call(f32[2,40,32,128]{3,2,1,0:T(8,128)S(1)} %get-tuple-element.5.act, bf16[2304,256]{1,0:T(8,128)(2,1)S(1)} %get-tuple-element.6.w, f32[3,32,16,256]{3,2,1,0:T(8,128)S(1)} %get-tuple-element.7.stage), custom_call_target="tpu_custom_call" | custom-call | tf_op jit(solution)/shard_map/pallas_call | solution.py:473
where the time goes:
time: 15.7 us; the launch traced here: 15.5 us
  Pallas kernels  14.9 us (95%)
  between operations  0.64 us (4%)
    pallas_call x1, Pallas kernels, two_sections(): pl.pallas_call(functools.partial(cycle_kernel, sizes), out_shape=(act, vm...  13.3 us
    pallas_call x1, Pallas kernels, two_sections(): pl.pallas_call(functools.partial(last_kernel, sizes[2]), out_shape=(jax.S...  1.56 us

commit v1 on v0

v1 whole, which is shorter than its diff:
```python
import functools

import jax
import jax.numpy as jnp
from jax import lax
from jax.experimental import pallas as pl
from jax.experimental.pallas import tpu as pltpu
from jax.sharding import PartitionSpec as P

MESH = pl.DeviceIdType.MESH
HALO = 4
LANES = 128
LIMIT = 32 * 1024 * 1024


def padded_2(shard, sides, width):
    for axis, dim in sides:
        size, length = (lax.axis_size(axis), shard.shape[dim])
        up = [(i, (i + 1) % size) for i in range(size - 1)]
        down = [(j, i) for i, j in up]
        last = lax.slice_in_dim(shard, length - width, length, axis=dim)
        initial = lax.slice_in_dim(shard, 0, width, axis=dim)
        before = lax.ppermute(last, axis, up)
        after = lax.ppermute(initial, axis, down)
        shard = jnp.concatenate([before, shard, after], axis=dim)
    return shard


def shifted_2(block, axis, distance):
    devices = range(lax.axis_size(axis))
    route = [(i - distance, i) for i in devices if i - distance in devices]
    return lax.ppermute(block, axis, route)


def activate(field):
    return jax.nn.silu(field).astype(jnp.bfloat16)


def apply_stencil(padded, flat_weight, out_rows, out_cols):
    channels = padded.shape[2]
    patches = jnp.concatenate(
        [
            padded[shift_row : shift_row + out_rows, shift_col : shift_col + out_cols]
            for shift_row in range(3)
            for shift_col in range(3)
        ],
        axis=2,
    )
    summed = jnp.dot(
        patches.reshape(out_rows * out_cols, 9 * channels),
        flat_weight,
        preferred_element_type=jnp.float32,
    )
    return summed.reshape(out_rows, out_cols, channels)


def section_pass(anchor, first_weight, second_weight, step_size):
    rows_here, cols_here, channels = anchor.shape
    widened = padded_2(anchor, (("rows", 0), ("cols", 1)), 2)
    slope_wide = apply_stencil(activate(widened), first_weight, rows_here + 2, cols_here + 2)
    middle_wide = widened[1:-1, 1:-1] + step_size * slope_wide
    row_global = lax.axis_index("rows") * rows_here - 1 + jnp.arange(rows_here + 2)
    col_global = lax.axis_index("cols") * cols_here - 1 + jnp.arange(cols_here + 2)
    inside_rows = (row_global >= 0) & (row_global < rows_here * lax.axis_size("rows"))
    inside_cols = (col_global >= 0) & (col_global < cols_here * lax.axis_size("cols"))
    inside = inside_rows[:, None] & inside_cols[None, :]
    second_act = jnp.where(inside[:, :, None], activate(middle_wide), jnp.zeros((), jnp.bfloat16))
    first_slope = slope_wide[1:-1, 1:-1]
    middle = middle_wide[1:-1, 1:-1]
    second_slope = apply_stencil(second_act, second_weight, rows_here, cols_here)
    ending = middle + step_size * second_slope
    return (first_slope, middle, ending)


def chain_on_device(section_states, weights):
    rows_here, cols_here, channels = section_states.shape[1:]
    ndepth = lax.axis_size("depth")
    position = lax.axis_index("depth")
    step_size = 2.0 / (2 * ndepth)
    first_weight = weights[0].reshape(9 * channels, channels)
    second_weight = weights[1].reshape(9 * channels, channels)
    anchor = section_states[0]
    first_slope, middle, ending = section_pass(anchor, first_weight, second_weight, step_size)
    jump = ending - (anchor + 2.0 * step_size * first_slope)

    def chain_turn(step_index, current):
        padded = padded_2(activate(current), (("rows", 0), ("cols", 1)), 1)
        advanced = (
            current
            + 2.0 * step_size * apply_stencil(padded, first_weight, rows_here, cols_here)
            + jump
        )
        shifted = shifted_2(advanced, "depth", 1)
        return jnp.where(position == 0, anchor, shifted)

    corrected = lax.fori_loop(0, ndepth - 1, chain_turn, anchor)
    final_slope, final_middle, final_ending = section_pass(
        corrected, first_weight, second_weight, step_size
    )
    fine_states = jnp.stack([final_middle, final_ending])
    return (fine_states, corrected[None])


DIRECTIONS = ((-1, 0), (1, 0), (0, -1), (0, 1), (-1, -1), (-1, 1), (1, -1), (1, 1))
LEFT = 8


def silu(u):
    half = 0.5 * u
    return half + half * jnp.tanh(half)


def masked_silu(u, mask):
    kept = (0.5 * u) * mask
    return kept + kept * jnp.tanh(0.5 * u)


def as_rows(block):
    return block.reshape(-1, LANES).astype(jnp.bfloat16)


def tap_dot(windows, halves, weight):
    lhs = []
    for a in range(3):
        for b in range(3):
            for c in range(halves):
                parts = [as_rows(window(c, a, b)) for window in windows]
                lhs.append(parts[0] if len(parts) == 1 else jnp.concatenate(parts, axis=0))
    return jnp.dot(jnp.concatenate(lhs, axis=1), weight[...], preferred_element_type=jnp.float32)


def lanes_of(block, c, shape):
    return block[:, c * LANES : (c + 1) * LANES].reshape(shape)


def upper_sublanes(rows):
    return lax.broadcasted_iota(jnp.int32, (rows, 8, LANES), 1) < HALO


def packed(ref, c, first_row, rows, left, right):
    near = ref[c, first_row : first_row + rows, left : left + 8, :]
    far = ref[c, first_row : first_row + rows, right : right + 8, :]
    return jnp.where(upper_sublanes(rows), near, far)


def store_packed(ref, c, first_row, left, right, value):
    whole = slice(first_row, first_row + value.shape[0])
    ref[c, whole, left : left + HALO, :] = value[:, 0:HALO]
    ref[c, whole, right + HALO : right + 8, :] = value[:, HALO:8]


def interior(layer, act, weight, before, after, act_after, step_size, shape):
    halves, rows_here, cols_here = shape
    first, rows = HALO + 1 + layer, rows_here - 2 - 2 * layer
    narrow = layer == 3 and cols_here == 16
    left, wide = (LEFT + HALO, cols_here - 2 * HALO) if narrow else (LEFT, cols_here)

    def window(c, a, b):
        return act[c, first + a - 1 : first + a - 1 + rows, left + b - 1 : left + b - 1 + wide, :]

    acc = step_size * tap_dot([window], halves, weight)
    for c in range(halves):
        here = (c, slice(first, first + rows), slice(left, left + wide), slice(None))
        u = before[here] + lanes_of(acc, c, (rows, wide, LANES))
        after[here] = u
        if act_after is not None:
            act_after[here] = silu(u)


def ring(layer, act, weight, before, after, act_after, step_size, shape, place):
    halves, rows_here, cols_here = shape
    nrows, ncols, row, col = place
    high = rows_here + 2 * HALO
    first, rows = 1 + layer, high - 2 - 2 * layer
    tops = (first, high - HALO - first)
    narrow = layer == 3 and cols_here == 16
    left, wide = (LEFT + HALO, cols_here - 2 * HALO) if narrow else (LEFT, cols_here)
    near, far = HALO + layer, LEFT + cols_here - 6 - layer

    def strip(at):
        return lambda c, a, b: act[c, at + a - 1 : at + a - 1 + HALO, left + b - 1 : left + b - 1 + wide, :]

    def sides(c, a, b):
        return packed(act, c, first + a - 1, rows, near + b, far + b)

    acc = step_size * tap_dot([strip(tops[0]), strip(tops[1]), sides], halves, weight)
    above = jnp.where(row > 0, 1.0, 0.0)
    below = jnp.where(row < nrows - 1, 1.0, 0.0)
    sub = lax.broadcasted_iota(jnp.int32, (1, 8, LANES), 1)
    j = jnp.where(sub < HALO, sub + (layer - 3), sub + (cols_here - 5 - layer)) + col * cols_here
    held = jnp.where((j >= 0) & (j < ncols * cols_here), 1.0, 0.0)
    m = HALO * wide
    for c in range(halves):
        for k, at in enumerate(tops):
            rise = lanes_of(acc[k * m : (k + 1) * m], c, (HALO, wide, LANES))
            here = (c, slice(at, at + HALO), slice(left, left + wide), slice(None))
            u = before[here] + rise
            after[here] = u
            if act_after is None:
                continue
            for i in range(HALO):
                value = silu(u[i])
                if at + i < HALO:
                    value = value * above
                elif at + i >= high - HALO:
                    value = value * below
                act_after[c, at + i, left : left + wide, :] = value
        u = packed(before, c, first, rows, near + 1, far + 1) + lanes_of(acc[2 * m :], c, (rows, 8, LANES))
        store_packed(after, c, first, near + 1, far + 1, u)
        if act_after is None:
            continue
        edge = HALO - first
        for at, n, mask in (
            (0, edge, held * above), (edge, rows - 2 * edge, held), (rows - edge, edge, held * below),
        ):
            if n > 0:
                store_packed(act_after, c, first + at, near + 1, far + 1, masked_silu(u[at : at + n], mask))


def gather_kernel(
    sizes, x_hbm, w_hbm,
    keep, mid, end, mid2, fin, act2, act3, w2, w3,
    base, land_mid, land_end, act0, act1, w0, w1, flat, send_row, send_col, recv_row, recv_side,
    load_sem, part_send, part_recv, pass_send, pass_recv, send_sem, recv_sem, later,
):
    nrows, ncols, step_size = sizes
    halves, high = base.shape[:2]
    rows_here, cols_here = keep.shape[:2]
    depth, row, col = lax.axis_index("depth"), lax.axis_index("rows"), lax.axis_index("cols")
    shape, place = (halves, rows_here, cols_here), (nrows, ncols, row, col)
    partner = (1 - depth, row, col)
    corner = HALO * HALO
    barrier = pltpu.get_barrier_semaphore()

    def lanes(c):
        return pl.ds(c * LANES, LANES)

    def local(src, dst, k):
        return pltpu.make_async_copy(src, dst, load_sem.at[k])

    def to_partner(src, dst, k, sems=(part_send, part_recv)):
        return pltpu.make_async_remote_copy(
            src_ref=src, dst_ref=dst, send_sem=sems[0].at[k], recv_sem=sems[1].at[k],
            device_id=partner, device_id_type=MESH,
        )

    def exists_at(step):
        there_row, there_col = row + step[0], col + step[1]
        exists = (there_row >= 0) & (there_row < nrows) & (there_col >= 0) & (there_col < ncols)
        return exists, there_row, there_col

    odd, even = lax.rem(row, 2) == 1, lax.rem(row, 2) == 0

    def pick(step, always, sometimes, first, second):
        if step == always:
            return True, None
        if step in sometimes:
            return first, second
        return None, True

    def early(step):
        return pick(step, (0, -1), ((-1, 0), (-1, -1)), odd, even)

    def early_seen_by(step):
        return pick(step, (0, 1), ((1, 0), (1, 1)), even, odd)

    def run_if(exists, also, action):
        if also is True:
            pl.when(exists)(action)
        elif also is not None:
            pl.when(exists)(lambda: pl.when(also)(action))

    def count_of(part):
        count = jnp.int32(1)
        for step in DIRECTIONS:
            also = early(step)[part]
            if also is not None:
                there = exists_at(step)[0]
                there = there if also is True else there & also
                count = count + jnp.where(there, 1, 0)
        return count

    def own(c):
        return base.at[c, pl.ds(HALO, rows_here), pl.ds(LEFT, cols_here), :]

    x_loads = [local(x_hbm.at[0, :, :, lanes(c)], own(c), c) for c in range(halves)]
    x_parts = [to_partner(x_hbm.at[0, :, :, lanes(c)], own(c), c) for c in range(halves)]
    keep_load = local(x_hbm.at[0], keep, halves + 2)
    w_loads = [local(w_hbm.at[0], w0, halves), local(w_hbm.at[1], w1, halves + 1)]
    late_loads = [local(w_hbm.at[0], w2, 0), local(w_hbm.at[1], w3, 1)]
    w_parts = [to_partner(w_hbm.at[0], w0, halves), to_partner(w_hbm.at[1], w1, halves + 1)]

    def inner(ref, k):
        return ref.at[:, pl.ds(HALO + k, rows_here - 2 * k), pl.ds(LEFT, cols_here), :]

    mid_part = to_partner(inner(mid, 1), inner(land_mid, 1), halves + 2)
    end_part = to_partner(inner(end, 2), inner(land_end, 2), halves + 3)
    passes = [
        to_partner(ref, ref, k, (pass_send, pass_recv)) for k, ref in enumerate((recv_row, recv_side))
    ]

    def activate_rows(source, target, first, rows, copied=None):
        def body(i, _):
            for c in range(halves):
                u = source[c, i, LEFT : LEFT + cols_here, :]
                target[c, i, LEFT : LEFT + cols_here, :] = silu(u)
                if copied is not None:
                    copied[c, i, LEFT : LEFT + cols_here, :] = u
            return 0

        lax.fori_loop(first, first + rows, body, 0, unroll=2)

    copies = []
    for k, (dr, dc) in enumerate(DIRECTIONS):
        exists, there_row, there_col = exists_at((dr, dc))
        side = (dc + 1) // 2
        mine = {-1: (0, corner), 1: ((rows_here - HALO) * HALO, corner), 0: (0, rows_here * HALO)}[dr]
        theirs = {1: (0, corner), -1: (high * HALO - corner, corner), 0: (corner, rows_here * HALO)}[dr]
        if dc == 0:
            src, dst, here = send_row.at[(dr + 1) // 2], recv_row.at[(1 - dr) // 2], recv_row.at[(dr + 1) // 2]
            empty = (recv_row, (dr + 1) // 2, slice(None))
        else:
            back = {-1: (0, corner), 1: (high * HALO - corner, corner), 0: (corner, rows_here * HALO)}[dr]
            src = send_col.at[side, pl.ds(*mine)]
            dst = recv_side.at[1 - side, pl.ds(*theirs)]
            here = recv_side.at[side, pl.ds(*back)]
            empty = (recv_side, side, slice(back[0], back[0] + back[1]))

        def remote(src, dst, slot):
            return pltpu.make_async_remote_copy(
                src_ref=src, dst_ref=dst, send_sem=send_sem.at[k], recv_sem=recv_sem.at[slot],
                device_id=(1 - depth, there_row, there_col), device_id_type=MESH,
            )

        opposite = DIRECTIONS.index((-dr, -dc))
        copies.append((exists, remote(src, dst, opposite), remote(src, here, k), empty))
    order = (4, 5, 6, 7, 2, 3, 0, 1)

    def signal(target):
        pl.semaphore_signal(barrier, inc=1, device_id=target, device_id_type=MESH)

    def send_halos(part):
        for k in order:
            exists, copy, _, _ = copies[k]
            run_if(exists, early(DIRECTIONS[k])[part], copy.start)

    @pl.when(depth == 0)
    def _():
        for copy in x_loads + w_loads:
            copy.start()
        signal(partner)
        pl.semaphore_wait(barrier, count_of(0))
        for copy in x_parts + w_parts[:1]:
            copy.start()
        for copy in x_loads:
            copy.wait()
        for side in range(2):
            top = HALO if side == 0 else rows_here
            left = LEFT if side == 0 else LEFT + cols_here - HALO
            for c in range(halves):
                send_row[side, :, lanes(c)] = as_rows(base[c, top : top + HALO, LEFT : LEFT + cols_here, :])
                for i in range(rows_here):
                    flat[side, c, i * HALO : (i + 1) * HALO, :] = base[c, HALO + i, left : left + HALO, :]
            for c in range(halves):
                send_col[side, :, lanes(c)] = flat[side, c, 0 : rows_here * HALO, :].astype(jnp.bfloat16)
        send_halos(0)
        activate_rows(base, act0, HALO, rows_here)
        w_loads[0].wait()
        interior(0, act0, w0, base, mid, act1, step_size, shape)
        mid_part.start()
        first = (row == 0) & (col == 0)

        def send_rest():
            pl.semaphore_wait(later.at[0], 1)
            send_halos(1)

        pl.when(row + col > 0)(send_rest)
        keep_load.start()
        w_loads[1].wait()
        interior(1, act1, w1, mid, end, act2, step_size, shape)
        end_part.start()
        pl.when(first)(send_rest)
        mid_part.wait_send()
        end_part.wait_send()
        w_parts[1].start()
        for copy in passes:
            copy.wait_recv()

    @pl.when(depth == 1)
    def _():
        for copy in late_loads:
            copy.start()
        signal(partner)
        for step in DIRECTIONS:
            exists, there_row, there_col = exists_at(step)
            for side, also in enumerate(early_seen_by(step)):
                core = 1 - depth if side == 0 else depth
                run_if(exists, also, functools.partial(signal, (core, there_row, there_col)))
        for step, (_, _, _, (ref, at, rows)) in zip(DIRECTIONS, copies):
            _, there_row, there_col = exists_at(step)
            outside = (there_row < 0) | (there_row >= nrows) | (there_col < 0) | (there_col >= ncols)

            @pl.when(outside)
            def _(ref=ref, at=at, rows=rows):
                ref[at, rows, :] = jnp.zeros_like(ref[at, rows, :])

        pl.semaphore_wait(barrier, count_of(1))
        pl.semaphore_signal(later.at[0], inc=1, device_id=partner, device_id_type=MESH)
        for copy in x_parts:
            copy.wait_recv()
        activate_rows(base, act0, HALO, rows_here)
        mid_part.wait_recv()
        activate_rows(land_mid, act1, HALO + 1, rows_here - 2, mid)
        end_part.wait_recv()
        activate_rows(land_end, act2, HALO + 2, rows_here - 4, end)
        late_loads[0].wait()
        interior(2, act2, w2, end, mid2, act3, step_size, shape)
        late_loads[1].wait()
        interior(3, act3, w3, mid2, fin, None, step_size, shape)
        for k in (0, 1, 2, 3, 4, 5, 6, 7):
            exists, _, arrival, _ = copies[k]
            pl.when(exists)(arrival.wait_recv)
        for copy in passes:
            copy.start()
        w_parts[0].wait_recv()

    for side in range(2):
        for c in range(halves):
            flat[side, c, 8 : 8 + high * HALO, :] = recv_side[side, :, lanes(c)].astype(jnp.float32)
            u = recv_row[side, :, lanes(c)].astype(jnp.float32).reshape(HALO, cols_here, LANES)
            rows = slice(0, HALO) if side == 0 else slice(high - HALO, high)
            base[c, rows, LEFT : LEFT + cols_here, :] = u
            act0[c, rows, LEFT : LEFT + cols_here, :] = silu(u)
    for i in range(high):
        for c in range(halves):
            at = 8 + i * HALO
            u = jnp.where(upper_sublanes(1)[0], flat[0, c, at : at + 8, :], flat[1, c, at - HALO : at + HALO, :])
            value = silu(u)
            for ref, v in ((base, u), (act0, value)):
                ref[c, i, LEFT - HALO : LEFT, :] = v[0:HALO]
                ref[c, i, LEFT + cols_here : LEFT + cols_here + HALO, :] = v[HALO:8]
    ring(0, act0, w0, base, mid, act1, step_size, shape, place)

    @pl.when(depth == 1)
    def _():
        w_parts[1].wait_recv()

    ring(1, act1, w1, mid, end, act2, step_size, shape, place)

    @pl.when(depth == 0)
    def _():
        keep_load.wait()
        for copy in x_parts + w_parts:
            copy.wait_send()
        for exists, copy, _, _ in copies:
            pl.when(exists)(copy.wait_send)

    @pl.when(depth == 1)
    def _():
        for copy in passes:
            copy.wait_send()


def ring_kernel(
    sizes, keep, mid, end, act2, w2, w3, mid2_in, fin_in, act3_in,
    fine_hbm, coarse_hbm, mid2, fin, act3, store_sem, keep_sem,
):
    nrows, ncols, step_size = sizes
    halves = end.shape[0]
    rows_here, cols_here = fine_hbm.shape[1:3]
    depth, row, col = lax.axis_index("depth"), lax.axis_index("rows"), lax.axis_index("cols")
    shape, place = (halves, rows_here, cols_here), (nrows, ncols, row, col)

    def stores(ref, target, slot):
        return [
            pltpu.make_async_copy(
                ref.at[c, pl.ds(HALO, rows_here), pl.ds(LEFT, cols_here), :],
                target.at[:, :, pl.ds(c * LANES, LANES)],
                store_sem.at[slot, c],
            )
            for c in range(halves)
        ]

    def start(copies):
        for copy in copies:
            copy.start()

    @pl.when(depth == 0)
    def _():
        kept = pltpu.make_async_copy(keep, coarse_hbm.at[0], keep_sem.at[0])
        both = stores(mid, fine_hbm.at[0], 0) + stores(end, fine_hbm.at[1], 1)
        start([kept] + both)
        for copy in [kept] + both:
            copy.wait()

    @pl.when(depth == 1)
    def _():
        early = stores(end, coarse_hbm.at[0], 0)
        start(early)
        ring(2, act2, w2, end, mid2, act3, step_size, shape, place)
        middle = stores(mid2, fine_hbm.at[0], 1)
        start(middle)
        ring(3, act3, w3, mid2, fin, None, step_size, shape, place)
        late = stores(fin, fine_hbm.at[1], 2)
        start(late)
        for copy in early + middle + late:
            copy.wait()


def two_sections(section_states, weights):
    _, rows_here, cols_here, channels = section_states.shape
    halves = channels // LANES
    high, wide = rows_here + 2 * HALO, cols_here + 2 * LEFT
    sizes = (lax.axis_size("rows"), lax.axis_size("cols"), 2.0 / (2 * lax.axis_size("depth")))
    f32, bf16, vmem = jnp.float32, jnp.bfloat16, pltpu.VMEM
    state = vmem((halves, high, wide, LANES), f32)
    weight = vmem((9 * channels, channels), bf16)
    flat_weights = weights.reshape(2, 9 * channels, channels)
    any_space, in_vmem = pl.BlockSpec(memory_space=pl.ANY), pl.BlockSpec(memory_space=vmem)
    dma = pltpu.SemaphoreType.DMA
    kept = vmem((rows_here, cols_here, channels), f32)
    keep, mid, end, mid2, fin, act2, act3, w2, w3 = pl.pallas_call(
        functools.partial(gather_kernel, sizes),
        out_shape=(kept,) + (state,) * 6 + (weight,) * 2,
        in_specs=[pl.BlockSpec(memory_space=pltpu.HBM)] * 2,
        out_specs=[in_vmem] * 9,
        scratch_shapes=[
            state, state, state, state, state, weight, weight,
            vmem((2, halves, high * HALO + 16, LANES), f32),
            vmem((2, HALO * cols_here, channels), bf16),
            vmem((2, rows_here * HALO, channels), bf16),
            vmem((2, HALO * cols_here, channels), bf16),
            vmem((2, high * HALO, channels), bf16),
            dma((halves + 3,)), dma((halves + 4,)), dma((halves + 4,)),
            dma((2,)), dma((2,)), dma((8,)), dma((8,)),
            pltpu.SemaphoreType.REGULAR((1,)),
        ],
        compiler_params=pltpu.CompilerParams(
            collective_id=0, has_side_effects=True, vmem_limit_bytes=LIMIT
        ),
    )(
        pltpu.with_memory_space_constraint(section_states, pltpu.HBM),
        pltpu.with_memory_space_constraint(flat_weights, pltpu.HBM),
    )
    outs = pl.pallas_call(
        functools.partial(ring_kernel, sizes),
        out_shape=(
            jax.ShapeDtypeStruct((2, rows_here, cols_here, channels), f32),
            jax.ShapeDtypeStruct((1, rows_here, cols_here, channels), f32),
        ) + (state,) * 3,
        in_specs=[in_vmem] * 9,
        out_specs=[any_space] * 2 + [in_vmem] * 3,
        input_output_aliases={6: 2, 7: 3, 8: 4},
        scratch_shapes=[dma((3, halves)), dma((1,))],
        compiler_params=pltpu.CompilerParams(vmem_limit_bytes=LIMIT),
    )(keep, mid, end, act2, w2, w3, mid2, fin, act3)
    return outs[0], outs[1]


def on_device(section_states, weights):
    _, rows_here, cols_here, channels = section_states.shape
    tiles = rows_here % 8 == 0 and cols_here % 8 == 0 and channels % LANES == 0
    if lax.axis_size("depth") == 2 and tiles and min(rows_here, cols_here) >= 16:
        return two_sections(section_states, weights)
    return chain_on_device(section_states, weights)


def solution(mesh):
    in_specs = (P("depth", "rows", "cols", None), P("depth", None, None, None, None))
    out_specs = (P("depth", "rows", "cols", None), P("depth", "rows", "cols", None))
    return jax.shard_map(
        on_device, mesh=mesh, in_specs=in_specs, out_specs=out_specs, check_vma=False
    )
```

time: 15.7 us -> 14.2 us (0.904)
  the two profiles are of different devices: /device:TPU:1 before, /device:TPU:3 now
where the time goes in v1:
time: 14.2 us; the launch traced here: 14 us
  Pallas kernels  13.4 us (94%)
  between operations  0.64 us (5%)
    pallas_call x1, Pallas kernels, two_sections(): pl.pallas_call(functools.partial(gather_kernel, sizes), out_shape=(kept,)...  10.5 us
    pallas_call x1, Pallas kernels, two_sections(): pl.pallas_call(functools.partial(ring_kernel, sizes), out_shape=(jax.Shap...  2.85 us

profile of v1, /device:TPU:3, one launch (start us, length us, event | category | flops | bytes accessed | tf_op | source)
XLA Modules:
  0.0 14.0 jit_solution(18242437992497314884)
XLA Ops:
  0.6 10.5 %shard_map.41 = (f32[32,16,256]{2,1,0:T(8,128)S(1)}, f32[2,40,32,128]{3,2,1,0:T(8,128)S(1)}, f32[2,40,32,128]{3,2,1,0:T(8,128)S(1)}, f32[2,40,32,128]{3,2,1,0:T(...) custom-call(f32[1,32,16,256]{3,2,1,0:T(8,128)} %x_hbm.1, ...), custom_call_target="tpu_custom_call" | custom-call | tf_op jit(solution)/shard_map/pallas_call | solution.py:522
  11.2 2.9 %shard_map.42 = (f32[2,32,16,256]{3,2,1,0:T(8,128)}, f32[1,32,16,256]{3,2,1,0:T(8,128)}, f32[2,40,32,128]{3,2,1,0:T(8,128)S(1)}, f32[2,40,32,128]{3,2,1,0:T(8,128)S(1)}, f32[2,40,32,128]{3,2,1,0:T(8,128)S(1)}) custom-call(f32[32,16,256]{2,1,0:T(8,128)S(1)} %get-tuple-element.13.keep, ...), custom_call_target="tpu_custom_call", output_to_operand_aliasing={{2}: (6, {}), {3}: (7, {}), {4}: (8, {})} | custom-call | tf_op jit(solution)/shard_map/pallas_call | solution.py:545

commit v2 on v1

--- a/solution.py
+++ b/solution.py
@@ -110,11 +110,6 @@
     return half + half * jnp.tanh(half)
 
 
-def masked_silu(u, mask):
-    kept = (0.5 * u) * mask
-    return kept + kept * jnp.tanh(0.5 * u)
-
-
 def as_rows(block):
     return block.reshape(-1, LANES).astype(jnp.bfloat16)
 
@@ -138,83 +133,94 @@
 
 
 def packed(ref, c, first_row, rows, left, right):
-    near = ref[c, first_row : first_row + rows, left : left + 8, :]
-    far = ref[c, first_row : first_row + rows, right : right + 8, :]
+    near = ref[c, pl.ds(first_row, rows), left : left + 8, :]
+    far = ref[c, pl.ds(first_row, rows), right : right + 8, :]
     return jnp.where(upper_sublanes(rows), near, far)
 
 
 def store_packed(ref, c, first_row, left, right, value):
-    whole = slice(first_row, first_row + value.shape[0])
+    whole = pl.ds(first_row, value.shape[0])
     ref[c, whole, left : left + HALO, :] = value[:, 0:HALO]
     ref[c, whole, right + HALO : right + 8, :] = value[:, HALO:8]
 
 
+def largest_divisor(total, limit):
+    return max(n for n in range(1, limit + 1) if total % n == 0)
+
+
 def interior(layer, act, weight, before, after, act_after, step_size, shape):
     halves, rows_here, cols_here = shape
-    first, rows = HALO + 1 + layer, rows_here - 2 - 2 * layer
     narrow = layer == 3 and cols_here == 16
     left, wide = (LEFT + HALO, cols_here - 2 * HALO) if narrow else (LEFT, cols_here)
-
-    def window(c, a, b):
-        return act[c, first + a - 1 : first + a - 1 + rows, left + b - 1 : left + b - 1 + wide, :]
-
-    acc = step_size * tap_dot([window], halves, weight)
-    for c in range(halves):
-        here = (c, slice(first, first + rows), slice(left, left + wide), slice(None))
-        u = before[here] + lanes_of(acc, c, (rows, wide, LANES))
-        after[here] = u
-        if act_after is not None:
-            act_after[here] = silu(u)
-
-
-def ring(layer, act, weight, before, after, act_after, step_size, shape, place):
+    exact = layer >= 2
+    first, rows = (HALO + 1 + layer, rows_here - 2 - 2 * layer) if exact else (HALO + 1, rows_here - 2)
+    n = rows if exact else largest_divisor(rows, 10)
+
+    def chunk(k, _):
+        at = first + k * n
+
+        def window(c, a, b):
+            return act[c, pl.ds(at + a - 1, n), left + b - 1 : left + b - 1 + wide, :]
+
+        acc = step_size * tap_dot([window], halves, weight)
+        for c in range(halves):
+            here = (c, pl.ds(at, n), slice(left, left + wide), slice(None))
+            u = before[here] + lanes_of(acc, c, (n, wide, LANES))
+            after[here] = u
+            if act_after is not None:
+                act_after[here] = silu(u)
+        return 0
+
+    lax.fori_loop(0, rows // n, chunk, 0)
+
+
+def ring(layer, act, weight, before, after, act_after, step_size, shape, place, done=None):
     halves, rows_here, cols_here = shape
     nrows, ncols, row, col = place
     high = rows_here + 2 * HALO
     first, rows = 1 + layer, high - 2 - 2 * layer
-    tops = (first, high - HALO - first)
+    n = (rows + 3) // 4 * 2
     narrow = layer == 3 and cols_here == 16
     left, wide = (LEFT + HALO, cols_here - 2 * HALO) if narrow else (LEFT, cols_here)
     near, far = HALO + layer, LEFT + cols_here - 6 - layer
-
-    def strip(at):
-        return lambda c, a, b: act[c, at + a - 1 : at + a - 1 + HALO, left + b - 1 : left + b - 1 + wide, :]
-
-    def sides(c, a, b):
-        return packed(act, c, first + a - 1, rows, near + b, far + b)
-
-    acc = step_size * tap_dot([strip(tops[0]), strip(tops[1]), sides], halves, weight)
     above = jnp.where(row > 0, 1.0, 0.0)
     below = jnp.where(row < nrows - 1, 1.0, 0.0)
     sub = lax.broadcasted_iota(jnp.int32, (1, 8, LANES), 1)
     j = jnp.where(sub < HALO, sub + (layer - 3), sub + (cols_here - 5 - layer)) + col * cols_here
     held = jnp.where((j >= 0) & (j < ncols * cols_here), 1.0, 0.0)
     m = HALO * wide
-    for c in range(halves):
-        for k, at in enumerate(tops):
-            rise = lanes_of(acc[k * m : (k + 1) * m], c, (HALO, wide, LANES))
-            here = (c, slice(at, at + HALO), slice(left, left + wide), slice(None))
-            u = before[here] + rise
+
+    def rows_held(at, block):
+        i = lax.broadcasted_iota(jnp.int32, block, 0) + at
+        return jnp.where(i < HALO, above, jnp.where(i >= high - HALO, below, 1.0))
+
+    def chunk(k, _):
+        top = first + k * (high - HALO - 2 * first)
+        at = first + k * (rows - n)
+
+        def strip(c, a, b):
+            return act[c, pl.ds(top + a - 1, HALO), left + b - 1 : left + b - 1 + wide, :]
+
+        def sides(c, a, b):
+            return packed(act, c, at + a - 1, n, near + b, far + b)
+
+        acc = step_size * tap_dot([strip, sides], halves, weight)
+        for c in range(halves):
+            here = (c, pl.ds(top, HALO), slice(left, left + wide), slice(None))
+            u = before[here] + lanes_of(acc[:m], c, (HALO, wide, LANES))
             after[here] = u
-            if act_after is None:
-                continue
-            for i in range(HALO):
-                value = silu(u[i])
-                if at + i < HALO:
-                    value = value * above
-                elif at + i >= high - HALO:
-                    value = value * below
-                act_after[c, at + i, left : left + wide, :] = value
-        u = packed(before, c, first, rows, near + 1, far + 1) + lanes_of(acc[2 * m :], c, (rows, 8, LANES))
-        store_packed(after, c, first, near + 1, far + 1, u)
-        if act_after is None:
-            continue
-        edge = HALO - first
-        for at, n, mask in (
-            (0, edge, held * above), (edge, rows - 2 * edge, held), (rows - edge, edge, held * below),
-        ):
-            if n > 0:
-                store_packed(act_after, c, first + at, near + 1, far + 1, masked_silu(u[at : at + n], mask))
+            if act_after is not None:
+                act_after[here] = silu(u) * rows_held(top, u.shape)
+            u = packed(before, c, at, n, near + 1, far + 1) + lanes_of(acc[m:], c, (n, 8, LANES))
+            store_packed(after, c, at, near + 1, far + 1, u)
+            if act_after is not None:
+                value = silu(u) * (held * rows_held(at, u.shape))
+                store_packed(act_after, c, at, near + 1, far + 1, value)
+        if done is not None:
+            done(k)
+        return 0
+
+    lax.fori_loop(0, 2, chunk, 0)
 
 
 def gather_kernel(
@@ -346,7 +352,7 @@
 
     @pl.when(depth == 0)
     def _():
-        for copy in x_loads + w_loads:
+        for copy in x_loads + w_loads[:1]:
             copy.start()
         signal(partner)
         pl.semaphore_wait(barrier, count_of(0))
@@ -354,6 +360,7 @@
             copy.start()
         for copy in x_loads:
             copy.wait()
+        w_loads[1].start()
         for side in range(2):
             top = HALO if side == 0 else rows_here
             left = LEFT if side == 0 else LEFT + cols_here - HALO
@@ -383,6 +390,11 @@
         mid_part.wait_send()
         end_part.wait_send()
         w_parts[1].start()
+        keep_load.wait()
+        for exists, copy, _, _ in copies:
+            pl.when(exists)(copy.wait_send)
+        for copy in x_parts + w_parts:
+            copy.wait_send()
         for copy in passes:
             copy.wait_recv()
 
@@ -444,26 +456,15 @@
     @pl.when(depth == 1)
     def _():
         w_parts[1].wait_recv()
-
-    ring(1, act1, w1, mid, end, act2, step_size, shape, place)
-
-    @pl.when(depth == 0)
-    def _():
-        keep_load.wait()
-        for copy in x_parts + w_parts:
-            copy.wait_send()
-        for exists, copy, _, _ in copies:
-            pl.when(exists)(copy.wait_send)
-
-    @pl.when(depth == 1)
-    def _():
         for copy in passes:
             copy.wait_send()
 
+    ring(1, act1, w1, mid, end, act2, step_size, shape, place)
+
 
 def ring_kernel(
     sizes, keep, mid, end, act2, w2, w3, mid2_in, fin_in, act3_in,
-    fine_hbm, coarse_hbm, mid2, fin, act3, store_sem, keep_sem,
+    fine_hbm, coarse_hbm, mid2, fin, act3, store_sem, keep_sem, late_sem,
 ):
     nrows, ncols, step_size = sizes
     halves = end.shape[0]
@@ -500,10 +501,21 @@
         ring(2, act2, w2, end, mid2, act3, step_size, shape, place)
         middle = stores(mid2, fine_hbm.at[0], 1)
         start(middle)
-        ring(3, act3, w3, mid2, fin, None, step_size, shape, place)
-        late = stores(fin, fine_hbm.at[1], 2)
-        start(late)
-        for copy in early + middle + late:
+
+        def late(k, c):
+            rows = rows_here // 2
+            return pltpu.make_async_copy(
+                fin.at[c, pl.ds(HALO + k * rows, rows), pl.ds(LEFT, cols_here), :],
+                fine_hbm.at[1, pl.ds(k * rows, rows), :, pl.ds(c * LANES, LANES)],
+                late_sem.at[k, c],
+            )
+
+        def send(k):
+            for c in range(halves):
+                late(k, c).start()
+
+        ring(3, act3, w3, mid2, fin, None, step_size, shape, place, send)
+        for copy in early + middle + [late(k, c) for k in range(2) for c in range(halves)]:
             copy.wait()
 
 
@@ -551,7 +563,7 @@
         in_specs=[in_vmem] * 9,
         out_specs=[any_space] * 2 + [in_vmem] * 3,
         input_output_aliases={6: 2, 7: 3, 8: 4},
-        scratch_shapes=[dma((3, halves)), dma((1,))],
+        scratch_shapes=[dma((2, halves)), dma((1,)), dma((2, halves))],
         compiler_params=pltpu.CompilerParams(vmem_limit_bytes=LIMIT),
     )(keep, mid, end, act2, w2, w3, mid2, fin, act3)
     return outs[0], outs[1]

time: 14.2 us -> 13.5 us (0.951)
  the two profiles are of different devices: /device:TPU:3 before, /device:TPU:25 now
where the time goes in v2:
time: 13.5 us; the launch traced here: 13.3 us
  Pallas kernels  12.7 us (94%)
  between operations  0.64 us (5%)
    pallas_call x1, Pallas kernels, two_sections(): pl.pallas_call(functools.partial(gather_kernel, sizes), out_shape=(kept,)...  10.1 us
    pallas_call x1, Pallas kernels, two_sections(): pl.pallas_call(functools.partial(ring_kernel, sizes), out_shape=(jax.Shap...  2.57 us

profile of v2, /device:TPU:25, one launch (start us, length us, event | category | flops | bytes accessed | tf_op | source)
XLA Modules:
  0.0 13.3 jit_solution(7819164124302836557)
XLA Ops:
  0.6 10.1 %shard_map.41 = (f32[32,16,256]{2,1,0:T(8,128)S(1)}, f32[2,40,32,128]{3,2,1,0:T(8,128)S(1)}, f32[2,40,32,128]{3,2,1,0:T(8,128)S(1)}, f32[2,40,32,128]{3,2,1,0:T(...) custom-call(f32[1,32,16,256]{3,2,1,0:T(8,128)} %x_hbm.1, ...), custom_call_target="tpu_custom_call" | custom-call | tf_op jit(solution)/shard_map/pallas_call | solution.py:534
  10.8 2.6 %shard_map.42 = (f32[2,32,16,256]{3,2,1,0:T(8,128)}, f32[1,32,16,256]{3,2,1,0:T(8,128)}, f32[2,40,32,128]{3,2,1,0:T(8,128)S(1)}, f32[2,40,32,128]{3,2,1,0:T(8,128)S(1)}, f32[2,40,32,128]{3,2,1,0:T(8,128)S(1)}) custom-call(f32[32,16,256]{2,1,0:T(8,128)S(1)} %get-tuple-element.13.keep, ...), custom_call_target="tpu_custom_call", output_to_operand_aliasing={{2}: (6, {}), {3}: (7, {}), {4}: (8, {})} | custom-call | tf_op jit(solution)/shard_map/pallas_call | solution.py:557

commit v3 on v2

--- a/solution.py
+++ b/solution.py
@@ -148,13 +148,17 @@
     return max(n for n in range(1, limit + 1) if total % n == 0)
 
 
+def once():
+    return jnp.minimum(lax.axis_index("rows"), 0) + 1
+
+
 def interior(layer, act, weight, before, after, act_after, step_size, shape):
     halves, rows_here, cols_here = shape
     narrow = layer == 3 and cols_here == 16
     left, wide = (LEFT + HALO, cols_here - 2 * HALO) if narrow else (LEFT, cols_here)
     exact = layer >= 2
     first, rows = (HALO + 1 + layer, rows_here - 2 - 2 * layer) if exact else (HALO + 1, rows_here - 2)
-    n = rows if exact else largest_divisor(rows, 10)
+    n = rows if exact else largest_divisor(rows, 30)
 
     def chunk(k, _):
         at = first + k * n
@@ -171,15 +175,15 @@
                 act_after[here] = silu(u)
         return 0
 
-    lax.fori_loop(0, rows // n, chunk, 0)
-
-
-def ring(layer, act, weight, before, after, act_after, step_size, shape, place, done=None):
+    lax.fori_loop(0, once() if rows == n else rows // n, chunk, 0)
+
+
+def ring(layer, act, weight, before, after, act_after, step_size, shape, place):
     halves, rows_here, cols_here = shape
     nrows, ncols, row, col = place
     high = rows_here + 2 * HALO
     first, rows = 1 + layer, high - 2 - 2 * layer
-    n = (rows + 3) // 4 * 2
+    tops = (first, high - HALO - first)
     narrow = layer == 3 and cols_here == 16
     left, wide = (LEFT + HALO, cols_here - 2 * HALO) if narrow else (LEFT, cols_here)
     near, far = HALO + layer, LEFT + cols_here - 6 - layer
@@ -194,43 +198,42 @@
         i = lax.broadcasted_iota(jnp.int32, block, 0) + at
         return jnp.where(i < HALO, above, jnp.where(i >= high - HALO, below, 1.0))
 
-    def chunk(k, _):
-        top = first + k * (high - HALO - 2 * first)
-        at = first + k * (rows - n)
-
-        def strip(c, a, b):
-            return act[c, pl.ds(top + a - 1, HALO), left + b - 1 : left + b - 1 + wide, :]
+    def whole(_, carry):
+        def strip(at):
+            return lambda c, a, b: act[c, pl.ds(at + a - 1, HALO), left + b - 1 : left + b - 1 + wide, :]
 
         def sides(c, a, b):
-            return packed(act, c, at + a - 1, n, near + b, far + b)
-
-        acc = step_size * tap_dot([strip, sides], halves, weight)
+            return packed(act, c, first + a - 1, rows, near + b, far + b)
+
+        acc = step_size * tap_dot([strip(at) for at in tops] + [sides], halves, weight)
         for c in range(halves):
-            here = (c, pl.ds(top, HALO), slice(left, left + wide), slice(None))
-            u = before[here] + lanes_of(acc[:m], c, (HALO, wide, LANES))
-            after[here] = u
+            for k, at in enumerate(tops):
+                here = (c, pl.ds(at, HALO), slice(left, left + wide), slice(None))
+                u = before[here] + lanes_of(acc[k * m : (k + 1) * m], c, (HALO, wide, LANES))
+                after[here] = u
+                if act_after is not None:
+                    act_after[here] = silu(u) * rows_held(at, u.shape)
+            u = packed(before, c, first, rows, near + 1, far + 1) + lanes_of(acc[2 * m :], c, (rows, 8, LANES))
+            store_packed(after, c, first, near + 1, far + 1, u)
             if act_after is not None:
-                act_after[here] = silu(u) * rows_held(top, u.shape)
-            u = packed(before, c, at, n, near + 1, far + 1) + lanes_of(acc[m:], c, (n, 8, LANES))
-            store_packed(after, c, at, near + 1, far + 1, u)
-            if act_after is not None:
-                value = silu(u) * (held * rows_held(at, u.shape))
-                store_packed(act_after, c, at, near + 1, far + 1, value)
-        if done is not None:
-            done(k)
-        return 0
-
-    lax.fori_loop(0, 2, chunk, 0)
+                value = silu(u) * (held * rows_held(first, u.shape))
+                store_packed(act_after, c, first, near + 1, far + 1, value)
+        return carry
+
+    lax.fori_loop(0, once(), whole, 0)
 
 
 def gather_kernel(
     sizes, x_hbm, w_hbm,
-    keep, mid, end, mid2, fin, act2, act3, w2, w3,
-    base, land_mid, land_end, act0, act1, w0, w1, flat, send_row, send_col, recv_row, recv_side,
-    load_sem, part_send, part_recv, pass_send, pass_recv, send_sem, recv_sem, later,
+    keep, states, mid2, fin, acts, act3, w2, w3,
+    land_mid, land_end, w01, flat, send_row, send_col, recv_row, recv_side,
+    load_sem, part_sem, pass_sem, halo_sem, later,
 ):
     nrows, ncols, step_size = sizes
-    halves, high = base.shape[:2]
+    base, mid, end = [states.at[k] for k in range(3)]
+    act0, act1, act2 = [acts.at[k] for k in range(3)]
+    w0, w1 = w01.at[0], w01.at[1]
+    halves, high = land_mid.shape[:2]
     rows_here, cols_here = keep.shape[:2]
     depth, row, col = lax.axis_index("depth"), lax.axis_index("rows"), lax.axis_index("cols")
     shape, place = (halves, rows_here, cols_here), (nrows, ncols, row, col)
@@ -244,9 +247,9 @@
     def local(src, dst, k):
         return pltpu.make_async_copy(src, dst, load_sem.at[k])
 
-    def to_partner(src, dst, k, sems=(part_send, part_recv)):
+    def to_partner(src, dst, k, sem=part_sem):
         return pltpu.make_async_remote_copy(
-            src_ref=src, dst_ref=dst, send_sem=sems[0].at[k], recv_sem=sems[1].at[k],
+            src_ref=src, dst_ref=dst, send_sem=sem.at[k], recv_sem=sem.at[k],
             device_id=partner, device_id_type=MESH,
         )
 
@@ -291,8 +294,8 @@
 
     x_loads = [local(x_hbm.at[0, :, :, lanes(c)], own(c), c) for c in range(halves)]
     x_parts = [to_partner(x_hbm.at[0, :, :, lanes(c)], own(c), c) for c in range(halves)]
-    keep_load = local(x_hbm.at[0], keep, halves + 2)
-    w_loads = [local(w_hbm.at[0], w0, halves), local(w_hbm.at[1], w1, halves + 1)]
+    keep_load = local(x_hbm.at[0], keep, 1)
+    w_loads = [local(w_hbm.at[0], w0, halves), local(w_hbm.at[1], w1, 0)]
     late_loads = [local(w_hbm.at[0], w2, 0), local(w_hbm.at[1], w3, 1)]
     w_parts = [to_partner(w_hbm.at[0], w0, halves), to_partner(w_hbm.at[1], w1, halves + 1)]
 
@@ -302,7 +305,7 @@
     mid_part = to_partner(inner(mid, 1), inner(land_mid, 1), halves + 2)
     end_part = to_partner(inner(end, 2), inner(land_end, 2), halves + 3)
     passes = [
-        to_partner(ref, ref, k, (pass_send, pass_recv)) for k, ref in enumerate((recv_row, recv_side))
+        to_partner(ref, ref, k, pass_sem) for k, ref in enumerate((recv_row, recv_side))
     ]
 
     def activate_rows(source, target, first, rows, copied=None):
@@ -334,7 +337,7 @@
 
         def remote(src, dst, slot):
             return pltpu.make_async_remote_copy(
-                src_ref=src, dst_ref=dst, send_sem=send_sem.at[k], recv_sem=recv_sem.at[slot],
+                src_ref=src, dst_ref=dst, send_sem=halo_sem.at[k], recv_sem=halo_sem.at[slot],
                 device_id=(1 - depth, there_row, there_col), device_id_type=MESH,
             )
 
@@ -373,18 +376,27 @@
         send_halos(0)
         activate_rows(base, act0, HALO, rows_here)
         w_loads[0].wait()
-        interior(0, act0, w0, base, mid, act1, step_size, shape)
-        mid_part.start()
         first = (row == 0) & (col == 0)
 
         def send_rest():
             pl.semaphore_wait(later.at[0], 1)
             send_halos(1)
 
-        pl.when(row + col > 0)(send_rest)
+        def both(layer, _):
+            @pl.when(layer == 1)
+            def _():
+                mid_part.start()
+                pl.when(row + col > 0)(send_rest)
+                w_loads[1].wait()
+
+            interior(
+                0, acts.at[layer], w01.at[layer], states.at[layer], states.at[layer + 1],
+                acts.at[layer + 1], step_size, shape,
+            )
+            return 0
+
+        lax.fori_loop(0, 2, both, 0)
         keep_load.start()
-        w_loads[1].wait()
-        interior(1, act1, w1, mid, end, act2, step_size, shape)
         end_part.start()
         pl.when(first)(send_rest)
         mid_part.wait_send()
@@ -463,11 +475,12 @@
 
 
 def ring_kernel(
-    sizes, keep, mid, end, act2, w2, w3, mid2_in, fin_in, act3_in,
-    fine_hbm, coarse_hbm, mid2, fin, act3, store_sem, keep_sem, late_sem,
+    sizes, keep, states, acts, w2, w3, mid2_in, fin_in, act3_in,
+    fine_hbm, coarse_hbm, mid2, fin, act3, store_sem,
 ):
     nrows, ncols, step_size = sizes
-    halves = end.shape[0]
+    mid, end, act2 = states.at[1], states.at[2], acts.at[2]
+    halves = fin.shape[0]
     rows_here, cols_here = fine_hbm.shape[1:3]
     depth, row, col = lax.axis_index("depth"), lax.axis_index("rows"), lax.axis_index("cols")
     shape, place = (halves, rows_here, cols_here), (nrows, ncols, row, col)
@@ -488,7 +501,7 @@
 
     @pl.when(depth == 0)
     def _():
-        kept = pltpu.make_async_copy(keep, coarse_hbm.at[0], keep_sem.at[0])
+        kept = pltpu.make_async_copy(keep, coarse_hbm.at[0], store_sem.at[2, 0])
         both = stores(mid, fine_hbm.at[0], 0) + stores(end, fine_hbm.at[1], 1)
         start([kept] + both)
         for copy in [kept] + both:
@@ -507,15 +520,19 @@
             return pltpu.make_async_copy(
                 fin.at[c, pl.ds(HALO + k * rows, rows), pl.ds(LEFT, cols_here), :],
                 fine_hbm.at[1, pl.ds(k * rows, rows), :, pl.ds(c * LANES, LANES)],
-                late_sem.at[k, c],
+                store_sem.at[2 * k, c],
             )
 
         def send(k):
             for c in range(halves):
                 late(k, c).start()
 
-        ring(3, act3, w3, mid2, fin, None, step_size, shape, place, send)
-        for copy in early + middle + [late(k, c) for k in range(2) for c in range(halves)]:
+        for copy in early:
+            copy.wait()
+        ring(3, act3, w3, mid2, fin, None, step_size, shape, place)
+        send(0)
+        send(1)
+        for copy in middle + [late(k, c) for k in range(2) for c in range(halves)]:
             copy.wait()
 
 
@@ -531,20 +548,20 @@
     any_space, in_vmem = pl.BlockSpec(memory_space=pl.ANY), pl.BlockSpec(memory_space=vmem)
     dma = pltpu.SemaphoreType.DMA
     kept = vmem((rows_here, cols_here, channels), f32)
-    keep, mid, end, mid2, fin, act2, act3, w2, w3 = pl.pallas_call(
+    three = vmem((3, halves, high, wide, LANES), f32)
+    keep, states, mid2, fin, acts, act3, w2, w3 = pl.pallas_call(
         functools.partial(gather_kernel, sizes),
-        out_shape=(kept,) + (state,) * 6 + (weight,) * 2,
+        out_shape=(kept, three, state, state, three, state, weight, weight),
         in_specs=[pl.BlockSpec(memory_space=pltpu.HBM)] * 2,
-        out_specs=[in_vmem] * 9,
+        out_specs=[in_vmem] * 8,
         scratch_shapes=[
-            state, state, state, state, state, weight, weight,
+            state, state, vmem((2, 9 * channels, channels), bf16),
             vmem((2, halves, high * HALO + 16, LANES), f32),
             vmem((2, HALO * cols_here, channels), bf16),
             vmem((2, rows_here * HALO, channels), bf16),
             vmem((2, HALO * cols_here, channels), bf16),
             vmem((2, high * HALO, channels), bf16),
-            dma((halves + 3,)), dma((halves + 4,)), dma((halves + 4,)),
-            dma((2,)), dma((2,)), dma((8,)), dma((8,)),
+            dma((halves + 1,)), dma((halves + 4,)), dma((2,)), dma((8,)),
             pltpu.SemaphoreType.REGULAR((1,)),
         ],
         compiler_params=pltpu.CompilerParams(
@@ -560,12 +577,12 @@
             jax.ShapeDtypeStruct((2, rows_here, cols_here, channels), f32),
             jax.ShapeDtypeStruct((1, rows_here, cols_here, channels), f32),
         ) + (state,) * 3,
-        in_specs=[in_vmem] * 9,
+        in_specs=[in_vmem] * 8,
         out_specs=[any_space] * 2 + [in_vmem] * 3,
-        input_output_aliases={6: 2, 7: 3, 8: 4},
-        scratch_shapes=[dma((2, halves)), dma((1,)), dma((2, halves))],
+        input_output_aliases={5: 2, 6: 3, 7: 4},
+        scratch_shapes=[dma((3, halves))],
         compiler_params=pltpu.CompilerParams(vmem_limit_bytes=LIMIT),
-    )(keep, mid, end, act2, w2, w3, mid2, fin, act3)
+    )(keep, states, acts, w2, w3, mid2, fin, act3)
     return outs[0], outs[1]
 
 

time: 13.5 us -> 12.1 us (0.90)
  the two profiles are of different devices: /device:TPU:25 before, /device:TPU:3 now
where the time goes in v3:
time: 12.1 us; the launch traced here: 11.9 us
  Pallas kernels  11.3 us (93%)
  between operations  0.64 us (5%)
    pallas_call x1, Pallas kernels, two_sections(): pl.pallas_call(functools.partial(gather_kernel, sizes), out_shape=(kept,...  8.99 us
    pallas_call x1, Pallas kernels, two_sections(): pl.pallas_call(functools.partial(ring_kernel, sizes), out_shape=(jax.Shap...  2.29 us

profile of v3, /device:TPU:3, one launch (start us, length us, event | category | flops | bytes accessed | tf_op | source)
XLA Modules:
  0.0 11.9 jit_solution(11905581376135966851)
XLA Ops:
  0.6 9.0 %shard_map.41 = (f32[32,16,256]{2,1,0:T(8,128)S(1)}, f32[3,2,40,32,128]{4,3,2,1,0:T(8,128)S(1)}, f32[2,40,32,128]{3,2,1,0:T(8,128)S(1)}, f32[2,40,32,128]{3,2,1,...) custom-call(f32[1,32,16,256]{3,2,1,0:T(8,128)} %x_hbm.1, ...), custom_call_target="tpu_custom_call" | custom-call | tf_op jit(solution)/shard_map/pallas_call | solution.py:552
  9.6 2.3 %shard_map.42 = (f32[2,32,16,256]{3,2,1,0:T(8,128)}, f32[1,32,16,256]{3,2,1,0:T(8,128)}, f32[2,40,32,128]{3,2,1,0:T(8,128)S(1)}, f32[2,40,32,128]{3,2,1,0:T(8,128)S(1)}, f32[2,40,32,128]{3,2,1,0:T(8,128)S(1)}) custom-call(f32[32,16,256]{2,1,0:T(8,128)S(1)} %get-tuple-element.12.keep, ...), custom_call_target="tpu_custom_call", output_to_operand_aliasing={{2}: (5, {}), {3}: (6, {}), {4}: (7, {})} | custom-call | tf_op jit(solution)/shard_map/pallas_call | solution.py:574

commit v4 on v3

--- a/solution.py
+++ b/solution.py
@@ -309,15 +309,12 @@
     ]
 
     def activate_rows(source, target, first, rows, copied=None):
-        def body(i, _):
-            for c in range(halves):
-                u = source[c, i, LEFT : LEFT + cols_here, :]
-                target[c, i, LEFT : LEFT + cols_here, :] = silu(u)
-                if copied is not None:
-                    copied[c, i, LEFT : LEFT + cols_here, :] = u
-            return 0
-
-        lax.fori_loop(first, first + rows, body, 0, unroll=2)
+        for c in range(halves):
+            here = (c, pl.ds(first, rows), slice(LEFT, LEFT + cols_here), slice(None))
+            u = source[here]
+            target[here] = silu(u)
+            if copied is not None:
+                copied[here] = u
 
     copies = []
     for k, (dr, dc) in enumerate(DIRECTIONS):
@@ -398,10 +395,10 @@
         lax.fori_loop(0, 2, both, 0)
         keep_load.start()
         end_part.start()
+        w_parts[1].start()
         pl.when(first)(send_rest)
         mid_part.wait_send()
         end_part.wait_send()
-        w_parts[1].start()
         keep_load.wait()
         for exists, copy, _, _ in copies:
             pl.when(exists)(copy.wait_send)
@@ -437,15 +434,18 @@
         activate_rows(land_mid, act1, HALO + 1, rows_here - 2, mid)
         end_part.wait_recv()
         activate_rows(land_end, act2, HALO + 2, rows_here - 4, end)
+        def forward():
+            for exists, _, arrival, _ in copies:
+                pl.when(exists)(arrival.wait_recv)
+            for copy in passes:
+                copy.start()
+
         late_loads[0].wait()
         interior(2, act2, w2, end, mid2, act3, step_size, shape)
+        pl.when((row == 0) & (col == 0))(forward)
         late_loads[1].wait()
         interior(3, act3, w3, mid2, fin, None, step_size, shape)
-        for k in (0, 1, 2, 3, 4, 5, 6, 7):
-            exists, _, arrival, _ = copies[k]
-            pl.when(exists)(arrival.wait_recv)
-        for copy in passes:
-            copy.start()
+        pl.when(row + col > 0)(forward)
         w_parts[0].wait_recv()
 
     for side in range(2):
@@ -468,10 +468,13 @@
     @pl.when(depth == 1)
     def _():
         w_parts[1].wait_recv()
+
+    ring(1, act1, w1, mid, end, act2, step_size, shape, place)
+
+    @pl.when(depth == 1)
+    def _():
         for copy in passes:
             copy.wait_send()
-
-    ring(1, act1, w1, mid, end, act2, step_size, shape, place)
 
 
 def ring_kernel(

time: 12.1 us -> 11.6 us (0.959)
  Pallas kernels: 11.3 us -> 10.8 us
    pallas_call x1, Pallas kernels: 8.99 us -> 8.47 us  [two_sections(): pl.pallas_call(functools.partial(gather_kernel, sizes), out_shape=(kept,...]
where the time goes in v4:
time: 11.6 us; the launch traced here: 11.4 us
  Pallas kernels  10.8 us (93%)
  between operations  0.64 us (6%)
    pallas_call x1, Pallas kernels, two_sections(): pl.pallas_call(functools.partial(gather_kernel, sizes), out_shape=(kept,...  8.47 us
    pallas_call x1, Pallas kernels, two_sections(): pl.pallas_call(functools.partial(ring_kernel, sizes), out_shape=(jax.Shap...  2.3 us

profile of v4, /device:TPU:3, one launch (start us, length us, event | category | flops | bytes accessed | tf_op | source)
XLA Modules:
  0.0 11.4 jit_solution(15266548844872642585)
XLA Ops:
  0.6 8.5 %shard_map.41 = (f32[32,16,256]{2,1,0:T(8,128)S(1)}, f32[3,2,40,32,128]{4,3,2,1,0:T(8,128)S(1)}, f32[2,40,32,128]{3,2,1,0:T(8,128)S(1)}, f32[2,40,32,128]{3,2,1,...) custom-call(f32[1,32,16,256]{3,2,1,0:T(8,128)} %x_hbm.1, ...), custom_call_target="tpu_custom_call" | custom-call | tf_op jit(solution)/shard_map/pallas_call | solution.py:555
  9.1 2.3 %shard_map.42 = (f32[2,32,16,256]{3,2,1,0:T(8,128)}, f32[1,32,16,256]{3,2,1,0:T(8,128)}, f32[2,40,32,128]{3,2,1,0:T(8,128)S(1)}, f32[2,40,32,128]{3,2,1,0:T(8,128)S(1)}, f32[2,40,32,128]{3,2,1,0:T(8,128)S(1)}) custom-call(f32[32,16,256]{2,1,0:T(8,128)S(1)} %get-tuple-element.12.keep, ...), custom_call_target="tpu_custom_call", output_to_operand_aliasing={{2}: (5, {}), {3}: (6, {}), {4}: (7, {})} | custom-call | tf_op jit(solution)/shard_map/pallas_call | solution.py:577

commit v5 on v4

--- a/solution.py
+++ b/solution.py
@@ -226,7 +226,7 @@
 def gather_kernel(
     sizes, x_hbm, w_hbm,
     keep, states, mid2, fin, acts, act3, w2, w3,
-    land_mid, land_end, w01, flat, send_row, send_col, recv_row, recv_side,
+    land_mid, land_end, w01, mid_side, land_side, flat, send_row, send_col, recv_row, recv_side,
     load_sem, part_sem, pass_sem, halo_sem, later,
 ):
     nrows, ncols, step_size = sizes
@@ -302,7 +302,14 @@
     def inner(ref, k):
         return ref.at[:, pl.ds(HALO + k, rows_here - 2 * k), pl.ds(LEFT, cols_here), :]
 
-    mid_part = to_partner(inner(mid, 1), inner(land_mid, 1), halves + 2)
+    def two_rows(ref, at):
+        return ref.at[:, pl.ds(at, 2), pl.ds(LEFT, cols_here), :]
+
+    edge_rows = (HALO + 1, HALO + rows_here - 3)
+    far_side = LEFT + cols_here - 8
+    mid_parts = [to_partner(mid_side, land_side, halves + 2)] + [
+        to_partner(two_rows(mid, at), two_rows(land_mid, at), halves + 4 + k) for k, at in enumerate(edge_rows)
+    ]
     end_part = to_partner(inner(end, 2), inner(land_end, 2), halves + 3)
     passes = [
         to_partner(ref, ref, k, pass_sem) for k, ref in enumerate((recv_row, recv_side))
@@ -382,7 +389,10 @@
         def both(layer, _):
             @pl.when(layer == 1)
             def _():
-                mid_part.start()
+                for c in range(halves):
+                    mid_side[c] = packed(mid, c, HALO + 1, rows_here - 2, LEFT, far_side)
+                for copy in mid_parts:
+                    copy.start()
                 pl.when(row + col > 0)(send_rest)
                 w_loads[1].wait()
 
@@ -397,7 +407,8 @@
         end_part.start()
         w_parts[1].start()
         pl.when(first)(send_rest)
-        mid_part.wait_send()
+        for copy in mid_parts:
+            copy.wait_send()
         end_part.wait_send()
         keep_load.wait()
         for exists, copy, _, _ in copies:
@@ -430,8 +441,14 @@
         for copy in x_parts:
             copy.wait_recv()
         activate_rows(base, act0, HALO, rows_here)
-        mid_part.wait_recv()
-        activate_rows(land_mid, act1, HALO + 1, rows_here - 2, mid)
+        for copy in mid_parts:
+            copy.wait_recv()
+        for at in edge_rows:
+            activate_rows(land_mid, act1, at, 2, mid)
+        for c in range(halves):
+            u = land_side[c]
+            store_packed(mid, c, HALO + 1, LEFT, far_side, u)
+            store_packed(act1, c, HALO + 1, LEFT, far_side, silu(u))
         end_part.wait_recv()
         activate_rows(land_end, act2, HALO + 2, rows_here - 4, end)
         def forward():
@@ -559,12 +576,13 @@
         out_specs=[in_vmem] * 8,
         scratch_shapes=[
             state, state, vmem((2, 9 * channels, channels), bf16),
+            vmem((halves, rows_here - 2, 8, LANES), f32), vmem((halves, rows_here - 2, 8, LANES), f32),
             vmem((2, halves, high * HALO + 16, LANES), f32),
             vmem((2, HALO * cols_here, channels), bf16),
             vmem((2, rows_here * HALO, channels), bf16),
             vmem((2, HALO * cols_here, channels), bf16),
             vmem((2, high * HALO, channels), bf16),
-            dma((halves + 1,)), dma((halves + 4,)), dma((2,)), dma((8,)),
+            dma((halves + 1,)), dma((halves + 6,)), dma((2,)), dma((8,)),
             pltpu.SemaphoreType.REGULAR((1,)),
         ],
         compiler_params=pltpu.CompilerParams(

time: 11.6 us -> 11.4 us (0.983)
  the two profiles are of different devices: /device:TPU:3 before, /device:TPU:1 now
where the time goes in v5:
time: 11.4 us; the launch traced here: 11.3 us
  Pallas kernels  10.6 us (93%)
  between operations  0.64 us (6%)
    pallas_call x1, Pallas kernels, two_sections(): pl.pallas_call(functools.partial(gather_kernel, sizes), out_shape=(kept,...  8.35 us
    pallas_call x1, Pallas kernels, two_sections(): pl.pallas_call(functools.partial(ring_kernel, sizes), out_shape=(jax.Shap...  2.29 us

profile of v5, /device:TPU:1, one launch (start us, length us, event | category | flops | bytes accessed | tf_op | source)
XLA Modules:
  0.0 11.3 jit_solution(10584315873894757650)
XLA Ops:
  0.6 8.4 %shard_map.41 = (f32[32,16,256]{2,1,0:T(8,128)S(1)}, f32[3,2,40,32,128]{4,3,2,1,0:T(8,128)S(1)}, f32[2,40,32,128]{3,2,1,0:T(8,128)S(1)}, f32[2,40,32,128]{3,2,1,...) custom-call(f32[1,32,16,256]{3,2,1,0:T(8,128)} %x_hbm.1, ...), custom_call_target="tpu_custom_call" | custom-call | tf_op jit(solution)/shard_map/pallas_call | solution.py:572
  9.0 2.3 %shard_map.42 = (f32[2,32,16,256]{3,2,1,0:T(8,128)}, f32[1,32,16,256]{3,2,1,0:T(8,128)}, f32[2,40,32,128]{3,2,1,0:T(8,128)S(1)}, f32[2,40,32,128]{3,2,1,0:T(8,128)S(1)}, f32[2,40,32,128]{3,2,1,0:T(8,128)S(1)}) custom-call(f32[32,16,256]{2,1,0:T(8,128)S(1)} %get-tuple-element.12.keep, ...), custom_call_target="tpu_custom_call", output_to_operand_aliasing={{2}: (5, {}), {3}: (6, {}), {4}: (7, {})} | custom-call | tf_op jit(solution)/shard_map/pallas_call | solution.py:595

commit v6 on v5

--- a/solution.py
+++ b/solution.py
@@ -535,24 +535,10 @@
         middle = stores(mid2, fine_hbm.at[0], 1)
         start(middle)
 
-        def late(k, c):
-            rows = rows_here // 2
-            return pltpu.make_async_copy(
-                fin.at[c, pl.ds(HALO + k * rows, rows), pl.ds(LEFT, cols_here), :],
-                fine_hbm.at[1, pl.ds(k * rows, rows), :, pl.ds(c * LANES, LANES)],
-                store_sem.at[2 * k, c],
-            )
-
-        def send(k):
-            for c in range(halves):
-                late(k, c).start()
-
-        for copy in early:
-            copy.wait()
         ring(3, act3, w3, mid2, fin, None, step_size, shape, place)
-        send(0)
-        send(1)
-        for copy in middle + [late(k, c) for k in range(2) for c in range(halves)]:
+        last = stores(fin, fine_hbm.at[1], 2)
+        start(last)
+        for copy in early + middle + last:
             copy.wait()
 
 

time: 11.4 us -> 11.4 us (level)
  no operation moved by 1% of the time
where the time goes in v6:
time: 11.4 us; the launch traced here: 11.2 us
  Pallas kernels  10.5 us (92%)
  between operations  0.64 us (6%)
    pallas_call x1, Pallas kernels, two_sections(): pl.pallas_call(functools.partial(gather_kernel, sizes), out_shape=(kept,...  8.35 us
    pallas_call x1, Pallas kernels, two_sections(): pl.pallas_call(functools.partial(ring_kernel, sizes), out_shape=(jax.Shap...  2.19 us

profile of v6, /device:TPU:1, one launch (start us, length us, event | category | flops | bytes accessed | tf_op | source)
XLA Modules:
  0.0 11.2 jit_solution(14458180302495064366)
XLA Ops:
  0.6 8.4 %shard_map.41 = (f32[32,16,256]{2,1,0:T(8,128)S(1)}, f32[3,2,40,32,128]{4,3,2,1,0:T(8,128)S(1)}, f32[2,40,32,128]{3,2,1,0:T(8,128)S(1)}, f32[2,40,32,128]{3,2,1,...) custom-call(f32[1,32,16,256]{3,2,1,0:T(8,128)} %x_hbm.1, ...), custom_call_target="tpu_custom_call" | custom-call | tf_op jit(solution)/shard_map/pallas_call | solution.py:558
  9.0 2.2 %shard_map.42 = (f32[2,32,16,256]{3,2,1,0:T(8,128)}, f32[1,32,16,256]{3,2,1,0:T(8,128)}, f32[2,40,32,128]{3,2,1,0:T(8,128)S(1)}, f32[2,40,32,128]{3,2,1,0:T(8,128)S(1)}, f32[2,40,32,128]{3,2,1,0:T(8,128)S(1)}) custom-call(f32[32,16,256]{2,1,0:T(8,128)S(1)} %get-tuple-element.12.keep, ...), custom_call_target="tpu_custom_call", output_to_operand_aliasing={{2}: (5, {}), {3}: (6, {}), {4}: (7, {})} | custom-call | tf_op jit(solution)/shard_map/pallas_call | solution.py:581

commit v7 on v6

--- a/solution.py
+++ b/solution.py
@@ -216,8 +216,13 @@
             u = packed(before, c, first, rows, near + 1, far + 1) + lanes_of(acc[2 * m :], c, (rows, 8, LANES))
             store_packed(after, c, first, near + 1, far + 1, u)
             if act_after is not None:
-                value = silu(u) * (held * rows_held(first, u.shape))
-                store_packed(act_after, c, first, near + 1, far + 1, value)
+                edge = HALO - first
+                for at, n, mask in (
+                    (0, edge, held * above), (edge, rows - 2 * edge, held), (rows - edge, edge, held * below),
+                ):
+                    if n > 0:
+                        value = silu(u[at : at + n]) * mask
+                        store_packed(act_after, c, first + at, near + 1, far + 1, value)
         return carry
 
     lax.fori_loop(0, once(), whole, 0)

time: 11.4 us -> 11.4 us (level)
  no operation moved by 1% of the time
where the time goes in v7:
time: 11.4 us; the launch traced here: 11.2 us
  Pallas kernels  10.5 us (92%)
  between operations  0.64 us (6%)
    pallas_call x1, Pallas kernels, two_sections(): pl.pallas_call(functools.partial(gather_kernel, sizes), out_shape=(kept,...  8.35 us
    pallas_call x1, Pallas kernels, two_sections(): pl.pallas_call(functools.partial(ring_kernel, sizes), out_shape=(jax.Shap...  2.19 us

profile of v7, /device:TPU:1, one launch (start us, length us, event | category | flops | bytes accessed | tf_op | source)
XLA Modules:
  0.0 11.2 jit_solution(2734301504985384656)
XLA Ops:
  0.6 8.4 %shard_map.41 = (f32[32,16,256]{2,1,0:T(8,128)S(1)}, f32[3,2,40,32,128]{4,3,2,1,0:T(8,128)S(1)}, f32[2,40,32,128]{3,2,1,0:T(8,128)S(1)}, f32[2,40,32,128]{3,2,1,...) custom-call(f32[1,32,16,256]{3,2,1,0:T(8,128)} %x_hbm.1, ...), custom_call_target="tpu_custom_call" | custom-call | tf_op jit(solution)/shard_map/pallas_call | solution.py:563
  9.0 2.2 %shard_map.42 = (f32[2,32,16,256]{3,2,1,0:T(8,128)}, f32[1,32,16,256]{3,2,1,0:T(8,128)}, f32[2,40,32,128]{3,2,1,0:T(8,128)S(1)}, f32[2,40,32,128]{3,2,1,0:T(8,128)S(1)}, f32[2,40,32,128]{3,2,1,0:T(8,128)S(1)}) custom-call(f32[32,16,256]{2,1,0:T(8,128)S(1)} %get-tuple-element.12.keep, ...), custom_call_target="tpu_custom_call", output_to_operand_aliasing={{2}: (5, {}), {3}: (6, {}), {4}: (7, {})} | custom-call | tf_op jit(solution)/shard_map/pallas_call | solution.py:586

commit v8 on v7

--- a/solution.py
+++ b/solution.py
@@ -194,10 +194,6 @@
     held = jnp.where((j >= 0) & (j < ncols * cols_here), 1.0, 0.0)
     m = HALO * wide
 
-    def rows_held(at, block):
-        i = lax.broadcasted_iota(jnp.int32, block, 0) + at
-        return jnp.where(i < HALO, above, jnp.where(i >= high - HALO, below, 1.0))
-
     def whole(_, carry):
         def strip(at):
             return lambda c, a, b: act[c, pl.ds(at + a - 1, HALO), left + b - 1 : left + b - 1 + wide, :]
@@ -212,7 +208,11 @@
                 u = before[here] + lanes_of(acc[k * m : (k + 1) * m], c, (HALO, wide, LANES))
                 after[here] = u
                 if act_after is not None:
-                    act_after[here] = silu(u) * rows_held(at, u.shape)
+                    value = silu(u)
+                    for i in range(HALO):
+                        held_row = above if at + i < HALO else below if at + i >= high - HALO else None
+                        row_value = value[i] if held_row is None else value[i] * held_row
+                        act_after[c, at + i, left : left + wide, :] = row_value
             u = packed(before, c, first, rows, near + 1, far + 1) + lanes_of(acc[2 * m :], c, (rows, 8, LANES))
             store_packed(after, c, first, near + 1, far + 1, u)
             if act_after is not None:

time: 11.4 us -> 11.4 us (level)
  no operation moved by 1% of the time
where the time goes in v8:
time: 11.4 us; the launch traced here: 11.2 us
  Pallas kernels  10.5 us (92%)
  between operations  0.64 us (6%)
    pallas_call x1, Pallas kernels, two_sections(): pl.pallas_call(functools.partial(gather_kernel, sizes), out_shape=(kept,...  8.35 us
    pallas_call x1, Pallas kernels, two_sections(): pl.pallas_call(functools.partial(ring_kernel, sizes), out_shape=(jax.Shap...  2.19 us

profile of v8, /device:TPU:1, one launch (start us, length us, event | category | flops | bytes accessed | tf_op | source)
XLA Modules:
  0.0 11.2 jit_solution(3430707779510592281)
XLA Ops:
  0.6 8.4 %shard_map.41 = (f32[32,16,256]{2,1,0:T(8,128)S(1)}, f32[3,2,40,32,128]{4,3,2,1,0:T(8,128)S(1)}, f32[2,40,32,128]{3,2,1,0:T(8,128)S(1)}, f32[2,40,32,128]{3,2,1,...) custom-call(f32[1,32,16,256]{3,2,1,0:T(8,128)} %x_hbm.1, ...), custom_call_target="tpu_custom_call" | custom-call | tf_op jit(solution)/shard_map/pallas_call | solution.py:563
  9.0 2.2 %shard_map.42 = (f32[2,32,16,256]{3,2,1,0:T(8,128)}, f32[1,32,16,256]{3,2,1,0:T(8,128)}, f32[2,40,32,128]{3,2,1,0:T(8,128)S(1)}, f32[2,40,32,128]{3,2,1,0:T(8,128)S(1)}, f32[2,40,32,128]{3,2,1,0:T(8,128)S(1)}) custom-call(f32[32,16,256]{2,1,0:T(8,128)S(1)} %get-tuple-element.12.keep, ...), custom_call_target="tpu_custom_call", output_to_operand_aliasing={{2}: (5, {}), {3}: (6, {}), {4}: (7, {})} | custom-call | tf_op jit(solution)/shard_map/pallas_call | solution.py:586
